TPU v7x, 32 devices: a whole 2x2x4 slice. The times are simulated.
32 devices in a mesh: dp: 2 (over x), lat: 4 (over y, core), lon: 4 (over z).
Axes of the slice: x: 2, y: 2, z: 4, core: 2. Of those that a mesh axis runs over, the one named last changes fastest.
Arguments:
- hidden_in: bfloat16 [2, 64, 512, 128], P('dp', 'lat', 'lon'), may hold values from -6 to 6
- conv_weight: bfloat16 [3, 3, 128, 128], replicated, may hold values from -0.1875 to 0.1875
- conv_bias: float32 [128], replicated, may hold values from -3 to 3
- proj_weight: float32 [128], replicated, may hold values from -5 to 5
- ocean_depth: float32 [64, 512], P('lat', 'lon'), may hold values from 0.5 to 2
- sea_mask: int32 [64, 512], P('lat', 'lon'), may hold values 0 or 1
- step_alpha: float32 [6], replicated, may hold values from 0.04 to 0.07
- step_beta: float32 [6], replicated, may hold values from 0.1 to 0.5
- surface_cotangent: float32 [2, 64, 512], P('dp', 'lat', 'lon'), may hold values from -20 to 20
Outputs:
- grad_hidden: bfloat16 [2, 64, 512, 128], P('dp', 'lat', 'lon')
- grad_weight: float32 [128, 3, 3, 128], P(('lat', 'lon'))
- grad_bias: float32 [128], replicated
- grad_proj: float32 [128], replicated
All inputs are finite; a program needn't handle non-finite values. No bound on the sum of `sea_mask` on one device may be relied on, other than what follows from the above.
Results may differ from a plain program's by a relative error of at most 0.01.
Values may be sent and summed in bfloat16 or wider, within the bound.
A program may use at most 64 MiB of HBM per device.

v0:
```python
import math
import jax
import jax.numpy as jnp
from jax import lax
from jax.sharding import PartitionSpec as P

ITERS = 6
helm_coef = 0.5


def extended(cells, sides, width, closed):
    for axis, dim in sides:
        count = lax.axis_size(axis)
        ends = count if closed else count - 1
        head = lax.slice_in_dim(cells, 0, width, axis=dim)
        tail = lax.slice_in_dim(cells, cells.shape[dim] - width, cells.shape[dim], axis=dim)
        cells = jnp.concatenate(
            [
                lax.ppermute(tail, axis, [(i, (i + 1) % count) for i in range(ends)]),
                cells,
                lax.ppermute(head, axis, [((i + 1) % count, i) for i in range(ends)]),
            ],
            axis=dim,
        )
    return cells


def operate(field_ext, mask_ext, depth_ext):
    rows_in = field_ext.shape[-2] - 2
    cols_in = field_ext.shape[-1] - 2
    center = field_ext[..., 1:-1, 1:-1]
    mask_mid = mask_ext[1:-1, 1:-1]
    depth_mid = depth_ext[1:-1, 1:-1]
    result = helm_coef * center
    for row_off, col_off in ((0, 1), (2, 1), (1, 0), (1, 2)):
        beside = field_ext[..., row_off : row_off + rows_in, col_off : col_off + cols_in]
        mask_near = mask_ext[row_off : row_off + rows_in, col_off : col_off + cols_in]
        depth_near = depth_ext[row_off : row_off + rows_in, col_off : col_off + cols_in]
        weight = mask_near * 0.5 * (depth_mid + depth_near)
        result = result + weight * (center - beside)
    return mask_mid * result


def solve_steps(adjoint_start, mask_ext, depth_ext, step_alpha, step_beta, widen):
    solution = jnp.zeros_like(adjoint_start)
    residual = adjoint_start
    direction = adjoint_start
    for turn_index in range(ITERS):
        solution = solution + step_alpha[turn_index] * direction
        if turn_index + 1 < ITERS:
            applied = operate(widen(direction), mask_ext, depth_ext)
            residual = residual - step_alpha[turn_index] * applied
            direction = residual + step_beta[turn_index] * direction
    return solution


def halo_field(field):
    field = extended(field, (("lat", 1),), 1, False)
    return extended(field, (("lon", 2),), 1, True)


def shards(
    hidden_in,
    conv_weight,
    conv_bias,
    proj_weight,
    ocean_depth,
    sea_mask,
    step_alpha,
    step_beta,
    surface_cotangent,
):
    samples, lat_rows, lon_cols, channels = hidden_in.shape
    mask_float = sea_mask.astype(jnp.float32)
    counted, summed = lax.psum(
        (jnp.sum(mask_float), jnp.sum(mask_float * surface_cotangent, axis=(1, 2))), ("lat", "lon")
    )
    adjoint_start = mask_float * (surface_cotangent - (summed / counted)[:, None, None])
    coefs = jnp.stack([mask_float, ocean_depth])
    coefs = extended(coefs, (("lat", 1),), 1, False)
    coefs = extended(coefs, (("lon", 2),), 1, True)
    solution = solve_steps(adjoint_start, coefs[0], coefs[1], step_alpha, step_beta, halo_field)
    forcing_grad = mask_float * solution
    padded = extended(hidden_in, (("lat", 1),), 1, False)
    padded = extended(padded, (("lon", 2),), 1, True)
    cell_count = samples * lat_rows * lon_cols
    shifted = [
        padded[:, row_off : row_off + lat_rows, col_off : col_off + lon_cols, :].reshape(
            cell_count, channels
        )
        for row_off in range(3)
        for col_off in range(3)
    ]
    preact = conv_bias
    for offset in range(9):
        preact = preact + jnp.dot(
            shifted[offset],
            conv_weight[offset // 3, offset % 3],
            preferred_element_type=jnp.float32,
        )
    sigma = jax.nn.sigmoid(preact)
    active = preact * sigma
    slope_act = sigma * (1.0 + preact * (1.0 - sigma))
    force_col = forcing_grad.reshape(cell_count)[:, None]
    grad_pre = (force_col * proj_weight * slope_act).astype(jnp.bfloat16)
    local_proj = jnp.sum(active * force_col, axis=0)
    local_bias = jnp.sum(grad_pre.astype(jnp.float32), axis=0)
    grad_ext = extended(
        grad_pre.reshape(samples, lat_rows, lon_cols, channels), (("lat", 1),), 1, False
    )
    grad_ext = extended(grad_ext, (("lon", 2),), 1, True)
    backed = jnp.zeros((cell_count, channels), jnp.float32)
    for row_off in range(3):
        for col_off in range(3):
            window = grad_ext[
                :, 2 - row_off : 2 - row_off + lat_rows, 2 - col_off : 2 - col_off + lon_cols, :
            ].reshape(cell_count, channels)
            backed = backed + lax.dot_general(
                window,
                conv_weight[row_off, col_off],
                (((1,), (1,)), ((), ())),
                preferred_element_type=jnp.float32,
            )
    grad_hidden = backed.reshape(samples, lat_rows, lon_cols, channels).astype(jnp.bfloat16)
    share = channels // lax.axis_size(("lat", "lon"))
    blocks = []
    for shifted_cols in shifted:
        blocks.append(
            lax.dot_general(
                shifted_cols, grad_pre, (((0,), (0,)), ((), ())), preferred_element_type=jnp.float32
            )
        )
    spatial = lax.psum_scatter(
        jnp.stack(blocks, axis=1).reshape(share * lax.axis_size(("lat", "lon")), 3, 3, channels),
        ("lat", "lon"),
        scatter_dimension=0,
        tiled=True,
    )
    own_weight = lax.psum(spatial, "dp")
    total_bias, total_proj = lax.psum((local_bias, local_proj), ("dp", "lat", "lon"))
    all_cells = cell_count * lax.axis_size("dp") * lax.axis_size("lat") * lax.axis_size("lon")
    grad_scale = 1.0 / math.sqrt(all_cells)
    return (grad_hidden, own_weight * grad_scale, total_bias * grad_scale, total_proj * grad_scale)


def solution(mesh):
    in_specs = (
        P("dp", "lat", "lon", None),
        P(),
        P(),
        P(),
        P("lat", "lon"),
        P("lat", "lon"),
        P(),
        P(),
        P("dp", "lat", "lon"),
    )
    out_specs = (P("dp", "lat", "lon", None), P(("lat", "lon"), None, None, None), P(), P())
    return jax.shard_map(shards, mesh=mesh, in_specs=in_specs, out_specs=out_specs, check_vma=False)
```

profile of v0, /device:TPU:0, one launch (start us, length us, event | category | flops | bytes accessed | tf_op | source)
XLA Modules:
  0.0 225.2 jit_solution(6670252528962750081)
XLA Ops:
  8.7 2.4 %collective-permute-start = (f32[2,1,128]{2,1,0:T(1,128)S(1)}, f32[2,1,128]{2,1,0:T(1,128)S(1)}, u32[]{:S(2)}, u32[]{:S(2)}) collective-permute-start(f32[2,1,128]{2,1,0:T(1,128)S(1)} %get-tuple-element.57), channel_id=1, source_target_pairs={{0,4},{4,8},{8,12},{1,5},{5,9},{9,13},{2,6},{6,10},{10,14},{3,7},{... | collective-permute-start | bytes 3080 | tf_op jit(solution)/shard_map/ppermute | solution.py:19
  11.1 1.3 collective-permute-start.1
  12.4 1.3 convert_reduce_fusion.1
  13.7 1.3 multiply_reduce_fusion.1
  15.0 36.6 %all-reduce.1 = (f32[1]{0:T(128)}, f32[1]{0:T(128)}) all-reduce(f32[1]{0:T(128)} %bitcast.2, f32[1]{0:T(128)} %bitcast.3), channel_id=1, replica_groups=mesh['dp'=2,'lat'=4,'lon'=4] {'lat','lon'}, use_global_device_ids=true, to_apply=%region_1.0 | all-reduce | flops 2 | bytes 16 | tf_op jit(solution)/shard_map/psum | solution.py:75
  53.6 1.3 collective-permute-start.4
  54.9 1.3 collective-permute-start.5
  56.2 1.5 fusion.171
  57.8 1.5 fusion.172
  61.0 3.7 %collective-permute-start.3 = (f32[2,18,1]{2,1,0:T(8,128)S(1)}, f32[2,18,1]{2,1,0:T(8,128)S(1)}, u32[]{:S(2)}, u32[]{:S(2)}) collective-permute-start(f32[2,18,1]{2,1,0:T(8,128)S(1)} %get-tuple-element.56), channel_id=1, source_target_pairs={{1,0},{2,1},{3,2},{0,3},{5,4},{6,5},{7,6},{4,7},{9,8},{10,9},{11,1... | collective-permute-start | bytes 440 | tf_op jit(solution)/shard_map/ppermute | solution.py:21
  64.7 2.0 collective-permute-start.7
  68.4 1.3 multiply_add_fusion.3
  69.7 2.6 %collective-permute-start.8 = (f32[1,1,128]{2,1,0:T(1,128)S(1)}, f32[1,1,128]{2,1,0:T(1,128)S(1)}, u32[]{:S(2)}, u32[]{:S(2)}) collective-permute-start(f32[1,1,128]{2,1,0:T(1,128)S(1)} %get-tuple-element.75), channel_id=1, source_target_pairs={{0,4},{4,8},{8,12},{1,5},{5,9},{9,13},{2,6},{6,10},{10,14},{3,7},{... | collective-permute-start | bytes 1544 | tf_op jit(solution)/shard_map/ppermute | solution.py:19
  72.3 1.3 collective-permute-start.9
  73.6 4.7 %collective-permute-done.9 = f32[1,1,128]{2,1,0:T(1,128)S(1)} collective-permute-done((f32[1,1,128]{2,1,0:T(1,128)S(1)}, f32[1,1,128]{2,1,0:T(1,128)S(1)}, u32[]{:S(2)}, u32[]{:S(2)}) %collective-permute-start.9) | collective-permute-done | bytes 544 | tf_op jit(solution)/shard_map/ppermute | solution.py:21
  78.4 3.8 %collective-permute-start.11 = (f32[1,18,1]{2,1,0:T(8,128)S(1)}, f32[1,18,1]{2,1,0:T(8,128)S(1)}, u32[]{:S(2)}, u32[]{:S(2)}) collective-permute-start(f32[1,18,1]{2,1,0:T(8,128)S(1)} %get-tuple-element.66), channel_id=1, source_target_pairs={{1,0},{2,1},{3,2},{0,3},{5,4},{6,5},{7,6},{4,7},{9,8},{10,9},{11,1... | collective-permute-start | bytes 224 | tf_op jit(solution)/shard_map/ppermute | solution.py:21
  82.2 1.7 collective-permute-done.10
  83.9 1.3 multiply_add_fusion.2
  85.2 3.3 %collective-permute-start.12 = (f32[1,1,128]{2,1,0:T(1,128)S(1)}, f32[1,1,128]{2,1,0:T(1,128)S(1)}, u32[]{:S(2)}, u32[]{:S(2)}) collective-permute-start(f32[1,1,128]{2,1,0:T(1,128)S(1)} %get-tuple-element.73), channel_id=1, source_target_pairs={{0,4},{4,8},{8,12},{1,5},{5,9},{9,13},{2,6},{6,10},{10,14},{3,7},{... | collective-permute-start | bytes 1544 | tf_op jit(solution)/shard_map/ppermute | solution.py:19
  88.6 1.3 collective-permute-start.13
  89.9 2.2 collective-permute-done.13
  93.3 2.8 %collective-permute-start.15 = (f32[1,18,1]{2,1,0:T(8,128)S(1)}, f32[1,18,1]{2,1,0:T(8,128)S(1)}, u32[]{:S(2)}, u32[]{:S(2)}) collective-permute-start(f32[1,18,1]{2,1,0:T(8,128)S(1)} %get-tuple-element.64), channel_id=1, source_target_pairs={{1,0},{2,1},{3,2},{0,3},{5,4},{6,5},{7,6},{4,7},{9,8},{10,9},{11,1... | collective-permute-start | bytes 224 | tf_op jit(solution)/shard_map/ppermute | solution.py:21
  96.1 1.6 collective-permute-done.14
  97.7 1.4 multiply_add_fusion.1
  99.0 3.4 %collective-permute-start.16 = (f32[1,1,128]{2,1,0:T(1,128)S(1)}, f32[1,1,128]{2,1,0:T(1,128)S(1)}, u32[]{:S(2)}, u32[]{:S(2)}) collective-permute-start(f32[1,1,128]{2,1,0:T(1,128)S(1)} %get-tuple-element.71), channel_id=1, source_target_pairs={{0,4},{4,8},{8,12},{1,5},{5,9},{9,13},{2,6},{6,10},{10,14},{3,7},{... | collective-permute-start | bytes 1544 | tf_op jit(solution)/shard_map/ppermute | solution.py:19
  102.4 1.3 collective-permute-start.17
  103.7 2.2 collective-permute-done.17
  106.0 1.3 collective-permute-start.18
  107.3 2.6 %collective-permute-start.19 = (f32[1,18,1]{2,1,0:T(8,128)S(1)}, f32[1,18,1]{2,1,0:T(8,128)S(1)}, u32[]{:S(2)}, u32[]{:S(2)}) collective-permute-start(f32[1,18,1]{2,1,0:T(8,128)S(1)} %get-tuple-element.62), channel_id=1, source_target_pairs={{1,0},{2,1},{3,2},{0,3},{5,4},{6,5},{7,6},{4,7},{9,8},{10,9},{11,1... | collective-permute-start | bytes 224 | tf_op jit(solution)/shard_map/ppermute | solution.py:21
  109.9 1.6 collective-permute-done.18
  111.5 1.3 multiply_add_fusion
  112.8 3.4 %collective-permute-start.20 = (f32[1,1,128]{2,1,0:T(1,128)S(1)}, f32[1,1,128]{2,1,0:T(1,128)S(1)}, u32[]{:S(2)}, u32[]{:S(2)}) collective-permute-start(f32[1,1,128]{2,1,0:T(1,128)S(1)} %get-tuple-element.69), channel_id=1, source_target_pairs={{0,4},{4,8},{8,12},{1,5},{5,9},{9,13},{2,6},{6,10},{10,14},{3,7},{... | collective-permute-start | bytes 1544 | tf_op jit(solution)/shard_map/ppermute | solution.py:19
  116.2 1.3 collective-permute-start.21
  117.5 3.5 %collective-permute-start.24 = (bf16[1,1,128,128]{3,2,1,0:T(8,128)(2,1)S(1)}, bf16[1,1,128,128]{3,2,1,0:T(8,128)(2,1)S(1)}, u32[]{:S(2)}, u32[]{:S(2)}) collective-permute-start(bf16[1,1,128,128]{3,2,1,0:T(8,128)(2,1)S(1)} %get-tuple-element.52), channel_id=1, source_target_pairs={{0,4},{4,8},{8,12},{1,5},{5,9},{9,13},{2,6},{6,10},{10,14},{3,7},{... | collective-permute-start | bytes 98312 | tf_op jit(solution)/shard_map/ppermute | solution.py:19
  121.0 1.3 collective-permute-start.25
  122.4 1.3 collective-permute-start.22
  123.7 2.6 %collective-permute-start.23 = (f32[1,18,1]{2,1,0:T(8,128)S(1)}, f32[1,18,1]{2,1,0:T(8,128)S(1)}, u32[]{:S(2)}, u32[]{:S(2)}) collective-permute-start(f32[1,18,1]{2,1,0:T(8,128)S(1)} %get-tuple-element.60), channel_id=1, source_target_pairs={{1,0},{2,1},{3,2},{0,3},{5,4},{6,5},{7,6},{4,7},{9,8},{10,9},{11,1... | collective-permute-start | bytes 224 | tf_op jit(solution)/shard_map/ppermute | solution.py:21
  126.3 1.6 collective-permute-done.22
  128.0 4.5 %fusion.69 = f32[2048]{0:T(1024)S(1)} fusion(f32[1,16,128]{2,1,0:T(8,128)S(1)} %get-tuple-element.11, f32[1,16,128]{2,1,0:T(8,128)S(1)} %get-tuple-element.21, f32[1,16,128]{2,1,0:T(8,128)S(1)} %get-tuple-element.10, f32[1,18,1]{2,1,0:T(8,128)S(1)} %collective-permute-done.23, f32[1,1,128]{2,1,0:T(1,128)S(1)} %collective-permute-done.21, ...), kind=kLoop, calls=%fused_computation.128 | loop fusion | flops 79872 | bytes 107692 | tf_op jit(solution)/shard_map/mul | solution.py:105
  132.9 1.4 collective-permute-start.26
  134.2 2.6 %collective-permute-start.27 = (bf16[1,18,1,128]{3,2,1,0:T(2,128)(2,1)S(1)}, bf16[1,18,1,128]{3,2,1,0:T(2,128)(2,1)S(1)}, u32[]{:S(2)}, u32[]{:S(2)}) collective-permute-start(bf16[1,18,1,128]{3,2,1,0:T(2,128)(2,1)S(1)} %get-tuple-element.43), channel_id=1, source_target_pairs={{1,0},{2,1},{3,2},{0,3},{5,4},{6,5},{7,6},{4,7},{9,8},{10,9},{11,1... | collective-permute-start | bytes 13832 | tf_op jit(solution)/shard_map/ppermute | solution.py:21
  137.1 1.3 collective-permute-done.26
  146.9 2.2 collective-permute-start.28
  149.1 1.3 collective-permute-start.29
  150.4 45.0 %all-reduce = (f32[128]{0:T(128)S(1)}, f32[128]{0:T(128)S(1)}) all-reduce(f32[128]{0:T(128)S(1)} %get-tuple-element.8, f32[128]{0:T(128)S(1)} %get-tuple-element.22), channel_id=1, replica_groups=mesh['dp'=2,'lat'=4,'lon'=4] {'dp','lat','lon'}, use_global_device_ids=true, to_apply=%region_7.0 | all-reduce | flops 256 | bytes 2048 | tf_op jit(solution)/shard_map/psum | solution.py:140
  196.0 2.4 %collective-permute-start.30 = (bf16[1,18,1,128]{3,2,1,0:T(2,128)(2,1)S(1)}, bf16[1,18,1,128]{3,2,1,0:T(2,128)(2,1)S(1)}, u32[]{:S(2)}, u32[]{:S(2)}) collective-permute-start(bf16[1,18,1,128]{3,2,1,0:T(2,128)(2,1)S(1)} %get-tuple-element.37), channel_id=1, source_target_pairs={{1,0},{2,1},{3,2},{0,3},{5,4},{6,5},{7,6},{4,7},{9,8},{10,9},{11,1... | collective-permute-start | bytes 13832 | tf_op jit(solution)/shard_map/ppermute | solution.py:21
  199.7 4.1 %collective-permute-done.31 = bf16[1,18,1,128]{3,2,1,0:T(2,128)(2,1)S(1)} collective-permute-done((bf16[1,18,1,128]{3,2,1,0:T(2,128)(2,1)S(1)}, bf16[1,18,1,128]{3,2,1,0:T(2,128)(2,1)S(1)}, u32[]{:S(2)}, u32[]{:S(2)}) %collective-permute-start.31) | collective-permute-done | bytes 4640 | tf_op jit(solution)/shard_map/ppermute | solution.py:19
  207.9 9.9 %psum.37 = f32[8,3,3,128]{3,0,2,1:T(8,128)S(1)} all-reduce(f32[8,3,3,128]{3,0,2,1:T(8,128)} %reduce-scatter.2.cloned.1.call-done), channel_id=1, replica_groups=mesh['dp'=2,'lat'=4,'lon'=4] {'dp'}, use_global_device_ids=true, to_apply=%region_5.0 | all-reduce | flops 9216 | bytes 73728 | tf_op jit(solution)/shard_map/psum | solution.py:139
  (105 shorter events, 22.7 us)
Async XLA Ops:
  7.2 120.8 %copy-start.3 = (s32[16,128]{1,0:T(8,128)S(1)}, s32[16,128]{1,0:T(8,128)}, u32[]{:S(2)}) copy-start(s32[16,128]{1,0:T(8,128)} %param.14) | copy-start | bytes 24580
  7.2 110.3 %copy-start = (bf16[1,16,128,128]{3,2,1,0:T(8,128)(2,1)S(1)}, bf16[1,16,128,128]{3,2,1,0:T(8,128)(2,1)}, u32[]{:S(2)}) copy-start(bf16[1,16,128,128]{3,2,1,0:T(8,128)(2,1)} %param.9) | copy-start | bytes 1572868
  7.2 200.7 %reduce-scatter.2.cloned.1.call-start = ((), (), s32[]{:S(2)}) async-start(), calls=%async_computation.1 | async-start | bytes 626688 | tf_op jit(solution)/shard_map/reduce_scatter | solution.py:133
  8.7 51.3 %collective-permute-start = (f32[2,1,128]{2,1,0:T(1,128)S(1)}, f32[2,1,128]{2,1,0:T(1,128)S(1)}, u32[]{:S(2)}, u32[]{:S(2)}) collective-permute-start(f32[2,1,128]{2,1,0:T(1,128)S(1)} %get-tuple-element.57), channel_id=1, source_target_pairs={{0,4},{4,8},{8,12},{1,5},{5,9},{9,13},{2,6},{6,10},{10,14},{3,7},{... | collective-permute-start | bytes 3080 | tf_op jit(solution)/shard_map/ppermute | solution.py:19
  11.1 49.0 %collective-permute-start.1 = (f32[2,1,128]{2,1,0:T(1,128)S(1)}, f32[2,1,128]{2,1,0:T(1,128)S(1)}, u32[]{:S(2)}, u32[]{:S(2)}) collective-permute-start(f32[2,1,128]{2,1,0:T(1,128)S(1)} %get-tuple-element.58), channel_id=1, source_target_pairs={{4,0},{8,4},{12,8},{5,1},{9,5},{13,9},{6,2},{10,6},{14,10},{7,3},{... | collective-permute-start | bytes 3080 | tf_op jit(solution)/shard_map/ppermute | solution.py:21
  53.6 5.6 %collective-permute-start.4 = (f32[1,1,128]{2,1,0:T(1,128)S(1)}, f32[1,1,128]{2,1,0:T(1,128)S(1)}, u32[]{:S(2)}, u32[]{:S(2)}) collective-permute-start(f32[1,1,128]{2,1,0:T(1,128)S(1)} %get-tuple-element.77), channel_id=1, source_target_pairs={{0,4},{4,8},{8,12},{1,5},{5,9},{9,13},{2,6},{6,10},{10,14},{3,7},{... | collective-permute-start | bytes 1544 | tf_op jit(solution)/shard_map/ppermute | solution.py:19
  54.9 5.0 %collective-permute-start.5 = (f32[1,1,128]{2,1,0:T(1,128)S(1)}, f32[1,1,128]{2,1,0:T(1,128)S(1)}, u32[]{:S(2)}, u32[]{:S(2)}) collective-permute-start(f32[1,1,128]{2,1,0:T(1,128)S(1)} %get-tuple-element.78), channel_id=1, source_target_pairs={{4,0},{8,4},{12,8},{5,1},{9,5},{13,9},{6,2},{10,6},{14,10},{7,3},{... | collective-permute-start | bytes 1544 | tf_op jit(solution)/shard_map/ppermute | solution.py:21
  60.0 7.5 %collective-permute-start.6 = (f32[1,18,1]{2,1,0:T(8,128)S(1)}, f32[1,18,1]{2,1,0:T(8,128)S(1)}, u32[]{:S(2)}, u32[]{:S(2)}) collective-permute-start(f32[1,18,1]{2,1,0:T(8,128)S(1)} %get-tuple-element.67), channel_id=1, source_target_pairs={{0,1},{1,2},{2,3},{3,0},{4,5},{5,6},{6,7},{7,4},{8,9},{9,10},{10,1... | collective-permute-start | bytes 224 | tf_op jit(solution)/shard_map/ppermute | solution.py:19
  60.8 5.8 %collective-permute-start.2 = (f32[2,18,1]{2,1,0:T(8,128)S(1)}, f32[2,18,1]{2,1,0:T(8,128)S(1)}, u32[]{:S(2)}, u32[]{:S(2)}) collective-permute-start(f32[2,18,1]{2,1,0:T(8,128)S(1)} %get-tuple-element.55), channel_id=1, source_target_pairs={{0,1},{1,2},{2,3},{3,0},{4,5},{5,6},{6,7},{7,4},{8,9},{9,10},{10,1... | collective-permute-start | bytes 440 | tf_op jit(solution)/shard_map/ppermute | solution.py:19
  61.0 5.7 %collective-permute-start.3 = (f32[2,18,1]{2,1,0:T(8,128)S(1)}, f32[2,18,1]{2,1,0:T(8,128)S(1)}, u32[]{:S(2)}, u32[]{:S(2)}) collective-permute-start(f32[2,18,1]{2,1,0:T(8,128)S(1)} %get-tuple-element.56), channel_id=1, source_target_pairs={{1,0},{2,1},{3,2},{0,3},{5,4},{6,5},{7,6},{4,7},{9,8},{10,9},{11,1... | collective-permute-start | bytes 440 | tf_op jit(solution)/shard_map/ppermute | solution.py:21
  64.7 3.7 %collective-permute-start.7 = (f32[1,18,1]{2,1,0:T(8,128)S(1)}, f32[1,18,1]{2,1,0:T(8,128)S(1)}, u32[]{:S(2)}, u32[]{:S(2)}) collective-permute-start(f32[1,18,1]{2,1,0:T(8,128)S(1)} %get-tuple-element.68), channel_id=1, source_target_pairs={{1,0},{2,1},{3,2},{0,3},{5,4},{6,5},{7,6},{4,7},{9,8},{10,9},{11,1... | collective-permute-start | bytes 224 | tf_op jit(solution)/shard_map/ppermute | solution.py:21
  69.7 3.9 %collective-permute-start.8 = (f32[1,1,128]{2,1,0:T(1,128)S(1)}, f32[1,1,128]{2,1,0:T(1,128)S(1)}, u32[]{:S(2)}, u32[]{:S(2)}) collective-permute-start(f32[1,1,128]{2,1,0:T(1,128)S(1)} %get-tuple-element.75), channel_id=1, source_target_pairs={{0,4},{4,8},{8,12},{1,5},{5,9},{9,13},{2,6},{6,10},{10,14},{3,7},{... | collective-permute-start | bytes 1544 | tf_op jit(solution)/shard_map/ppermute | solution.py:19
  72.3 6.0 %collective-permute-start.9 = (f32[1,1,128]{2,1,0:T(1,128)S(1)}, f32[1,1,128]{2,1,0:T(1,128)S(1)}, u32[]{:S(2)}, u32[]{:S(2)}) collective-permute-start(f32[1,1,128]{2,1,0:T(1,128)S(1)} %get-tuple-element.76), channel_id=1, source_target_pairs={{4,0},{8,4},{12,8},{5,1},{9,5},{13,9},{6,2},{10,6},{14,10},{7,3},{... | collective-permute-start | bytes 1544 | tf_op jit(solution)/shard_map/ppermute | solution.py:21
  78.4 5.5 %collective-permute-start.10 = (f32[1,18,1]{2,1,0:T(8,128)S(1)}, f32[1,18,1]{2,1,0:T(8,128)S(1)}, u32[]{:S(2)}, u32[]{:S(2)}) collective-permute-start(f32[1,18,1]{2,1,0:T(8,128)S(1)} %get-tuple-element.65), channel_id=1, source_target_pairs={{0,1},{1,2},{2,3},{3,0},{4,5},{5,6},{6,7},{7,4},{8,9},{9,10},{10,1... | collective-permute-start | bytes 224 | tf_op jit(solution)/shard_map/ppermute | solution.py:19
  78.4 5.5 %collective-permute-start.11 = (f32[1,18,1]{2,1,0:T(8,128)S(1)}, f32[1,18,1]{2,1,0:T(8,128)S(1)}, u32[]{:S(2)}, u32[]{:S(2)}) collective-permute-start(f32[1,18,1]{2,1,0:T(8,128)S(1)} %get-tuple-element.66), channel_id=1, source_target_pairs={{1,0},{2,1},{3,2},{0,3},{5,4},{6,5},{7,6},{4,7},{9,8},{10,9},{11,1... | collective-permute-start | bytes 224 | tf_op jit(solution)/shard_map/ppermute | solution.py:21
  85.2 4.6 %collective-permute-start.12 = (f32[1,1,128]{2,1,0:T(1,128)S(1)}, f32[1,1,128]{2,1,0:T(1,128)S(1)}, u32[]{:S(2)}, u32[]{:S(2)}) collective-permute-start(f32[1,1,128]{2,1,0:T(1,128)S(1)} %get-tuple-element.73), channel_id=1, source_target_pairs={{0,4},{4,8},{8,12},{1,5},{5,9},{9,13},{2,6},{6,10},{10,14},{3,7},{... | collective-permute-start | bytes 1544 | tf_op jit(solution)/shard_map/ppermute | solution.py:19
  88.6 3.5 %collective-permute-start.13 = (f32[1,1,128]{2,1,0:T(1,128)S(1)}, f32[1,1,128]{2,1,0:T(1,128)S(1)}, u32[]{:S(2)}, u32[]{:S(2)}) collective-permute-start(f32[1,1,128]{2,1,0:T(1,128)S(1)} %get-tuple-element.74), channel_id=1, source_target_pairs={{4,0},{8,4},{12,8},{5,1},{9,5},{13,9},{6,2},{10,6},{14,10},{7,3},{... | collective-permute-start | bytes 1544 | tf_op jit(solution)/shard_map/ppermute | solution.py:21
  92.2 5.5 %collective-permute-start.14 = (f32[1,18,1]{2,1,0:T(8,128)S(1)}, f32[1,18,1]{2,1,0:T(8,128)S(1)}, u32[]{:S(2)}, u32[]{:S(2)}) collective-permute-start(f32[1,18,1]{2,1,0:T(8,128)S(1)} %get-tuple-element.63), channel_id=1, source_target_pairs={{0,1},{1,2},{2,3},{3,0},{4,5},{5,6},{6,7},{7,4},{8,9},{9,10},{10,1... | collective-permute-start | bytes 224 | tf_op jit(solution)/shard_map/ppermute | solution.py:19
  93.3 4.4 %collective-permute-start.15 = (f32[1,18,1]{2,1,0:T(8,128)S(1)}, f32[1,18,1]{2,1,0:T(8,128)S(1)}, u32[]{:S(2)}, u32[]{:S(2)}) collective-permute-start(f32[1,18,1]{2,1,0:T(8,128)S(1)} %get-tuple-element.64), channel_id=1, source_target_pairs={{1,0},{2,1},{3,2},{0,3},{5,4},{6,5},{7,6},{4,7},{9,8},{10,9},{11,1... | collective-permute-start | bytes 224 | tf_op jit(solution)/shard_map/ppermute | solution.py:21
  99.0 4.7 %collective-permute-start.16 = (f32[1,1,128]{2,1,0:T(1,128)S(1)}, f32[1,1,128]{2,1,0:T(1,128)S(1)}, u32[]{:S(2)}, u32[]{:S(2)}) collective-permute-start(f32[1,1,128]{2,1,0:T(1,128)S(1)} %get-tuple-element.71), channel_id=1, source_target_pairs={{0,4},{4,8},{8,12},{1,5},{5,9},{9,13},{2,6},{6,10},{10,14},{3,7},{... | collective-permute-start | bytes 1544 | tf_op jit(solution)/shard_map/ppermute | solution.py:19
  102.4 3.5 %collective-permute-start.17 = (f32[1,1,128]{2,1,0:T(1,128)S(1)}, f32[1,1,128]{2,1,0:T(1,128)S(1)}, u32[]{:S(2)}, u32[]{:S(2)}) collective-permute-start(f32[1,1,128]{2,1,0:T(1,128)S(1)} %get-tuple-element.72), channel_id=1, source_target_pairs={{4,0},{8,4},{12,8},{5,1},{9,5},{13,9},{6,2},{10,6},{14,10},{7,3},{... | collective-permute-start | bytes 1544 | tf_op jit(solution)/shard_map/ppermute | solution.py:21
  106.0 5.5 %collective-permute-start.18 = (f32[1,18,1]{2,1,0:T(8,128)S(1)}, f32[1,18,1]{2,1,0:T(8,128)S(1)}, u32[]{:S(2)}, u32[]{:S(2)}) collective-permute-start(f32[1,18,1]{2,1,0:T(8,128)S(1)} %get-tuple-element.61), channel_id=1, source_target_pairs={{0,1},{1,2},{2,3},{3,0},{4,5},{5,6},{6,7},{7,4},{8,9},{9,10},{10,1... | collective-permute-start | bytes 224 | tf_op jit(solution)/shard_map/ppermute | solution.py:19
  107.3 4.2 %collective-permute-start.19 = (f32[1,18,1]{2,1,0:T(8,128)S(1)}, f32[1,18,1]{2,1,0:T(8,128)S(1)}, u32[]{:S(2)}, u32[]{:S(2)}) collective-permute-start(f32[1,18,1]{2,1,0:T(8,128)S(1)} %get-tuple-element.62), channel_id=1, source_target_pairs={{1,0},{2,1},{3,2},{0,3},{5,4},{6,5},{7,6},{4,7},{9,8},{10,9},{11,1... | collective-permute-start | bytes 224 | tf_op jit(solution)/shard_map/ppermute | solution.py:21
  112.8 9.5 %collective-permute-start.20 = (f32[1,1,128]{2,1,0:T(1,128)S(1)}, f32[1,1,128]{2,1,0:T(1,128)S(1)}, u32[]{:S(2)}, u32[]{:S(2)}) collective-permute-start(f32[1,1,128]{2,1,0:T(1,128)S(1)} %get-tuple-element.69), channel_id=1, source_target_pairs={{0,4},{4,8},{8,12},{1,5},{5,9},{9,13},{2,6},{6,10},{10,14},{3,7},{... | collective-permute-start | bytes 1544 | tf_op jit(solution)/shard_map/ppermute | solution.py:19
  116.2 6.1 %collective-permute-start.21 = (f32[1,1,128]{2,1,0:T(1,128)S(1)}, f32[1,1,128]{2,1,0:T(1,128)S(1)}, u32[]{:S(2)}, u32[]{:S(2)}) collective-permute-start(f32[1,1,128]{2,1,0:T(1,128)S(1)} %get-tuple-element.70), channel_id=1, source_target_pairs={{4,0},{8,4},{12,8},{5,1},{9,5},{13,9},{6,2},{10,6},{14,10},{7,3},{... | collective-permute-start | bytes 1544 | tf_op jit(solution)/shard_map/ppermute | solution.py:21
  117.5 14.9 %collective-permute-start.24 = (bf16[1,1,128,128]{3,2,1,0:T(8,128)(2,1)S(1)}, bf16[1,1,128,128]{3,2,1,0:T(8,128)(2,1)S(1)}, u32[]{:S(2)}, u32[]{:S(2)}) collective-permute-start(bf16[1,1,128,128]{3,2,1,0:T(8,128)(2,1)S(1)} %get-tuple-element.52), channel_id=1, source_target_pairs={{0,4},{4,8},{8,12},{1,5},{5,9},{9,13},{2,6},{6,10},{10,14},{3,7},{... | collective-permute-start | bytes 98312 | tf_op jit(solution)/shard_map/ppermute | solution.py:19
  121.0 11.5 %collective-permute-start.25 = (bf16[1,1,128,128]{3,2,1,0:T(8,128)(2,1)S(1)}, bf16[1,1,128,128]{3,2,1,0:T(8,128)(2,1)S(1)}, u32[]{:S(2)}, u32[]{:S(2)}) collective-permute-start(bf16[1,1,128,128]{3,2,1,0:T(8,128)(2,1)S(1)} %get-tuple-element.51), channel_id=1, source_target_pairs={{4,0},{8,4},{12,8},{5,1},{9,5},{13,9},{6,2},{10,6},{14,10},{7,3},{... | collective-permute-start | bytes 98312 | tf_op jit(solution)/shard_map/ppermute | solution.py:21
  122.4 5.5 %collective-permute-start.22 = (f32[1,18,1]{2,1,0:T(8,128)S(1)}, f32[1,18,1]{2,1,0:T(8,128)S(1)}, u32[]{:S(2)}, u32[]{:S(2)}) collective-permute-start(f32[1,18,1]{2,1,0:T(8,128)S(1)} %get-tuple-element.59), channel_id=1, source_target_pairs={{0,1},{1,2},{2,3},{3,0},{4,5},{5,6},{6,7},{7,4},{8,9},{9,10},{10,1... | collective-permute-start | bytes 224 | tf_op jit(solution)/shard_map/ppermute | solution.py:19
  123.7 4.2 %collective-permute-start.23 = (f32[1,18,1]{2,1,0:T(8,128)S(1)}, f32[1,18,1]{2,1,0:T(8,128)S(1)}, u32[]{:S(2)}, u32[]{:S(2)}) collective-permute-start(f32[1,18,1]{2,1,0:T(8,128)S(1)} %get-tuple-element.60), channel_id=1, source_target_pairs={{1,0},{2,1},{3,2},{0,3},{5,4},{6,5},{7,6},{4,7},{9,8},{10,9},{11,1... | collective-permute-start | bytes 224 | tf_op jit(solution)/shard_map/ppermute | solution.py:21
  132.5 4.4 %copy-start.1 = (bf16[3,3,128,128]{3,2,1,0:T(8,128)(2,1)S(1)}, bf16[3,3,128,128]{3,2,1,0:T(8,128)(2,1)}, u32[]{:S(2)}) copy-start(bf16[3,3,128,128]{3,2,1,0:T(8,128)(2,1)} %param.10) | copy-start | bytes 884740
  132.9 5.6 %collective-permute-start.26 = (bf16[1,18,1,128]{3,2,1,0:T(2,128)(2,1)S(1)}, bf16[1,18,1,128]{3,2,1,0:T(2,128)(2,1)S(1)}, u32[]{:S(2)}, u32[]{:S(2)}) collective-permute-start(bf16[1,18,1,128]{3,2,1,0:T(2,128)(2,1)S(1)} %get-tuple-element.42), channel_id=1, source_target_pairs={{0,1},{1,2},{2,3},{3,0},{4,5},{5,6},{6,7},{7,4},{8,9},{9,10},{10,1... | collective-permute-start | bytes 13832 | tf_op jit(solution)/shard_map/ppermute | solution.py:19
  134.2 4.2 %collective-permute-start.27 = (bf16[1,18,1,128]{3,2,1,0:T(2,128)(2,1)S(1)}, bf16[1,18,1,128]{3,2,1,0:T(2,128)(2,1)S(1)}, u32[]{:S(2)}, u32[]{:S(2)}) collective-permute-start(bf16[1,18,1,128]{3,2,1,0:T(2,128)(2,1)S(1)} %get-tuple-element.43), channel_id=1, source_target_pairs={{1,0},{2,1},{3,2},{0,3},{5,4},{6,5},{7,6},{4,7},{9,8},{10,9},{11,1... | collective-permute-start | bytes 13832 | tf_op jit(solution)/shard_map/ppermute | solution.py:21
  139.6 0.7 copy-start.4
  141.4 0.7 copy-start.5
  146.0 0.8 copy-start.2
  146.9 49.1 %collective-permute-start.28 = (bf16[1,1,128,128]{3,2,1,0:T(8,128)(2,1)S(1)}, bf16[1,1,128,128]{3,2,1,0:T(8,128)(2,1)S(1)}, u32[]{:S(2)}, u32[]{:S(2)}) collective-permute-start(bf16[1,1,128,128]{3,2,1,0:T(8,128)(2,1)S(1)} %get-tuple-element.46), channel_id=1, source_target_pairs={{0,4},{4,8},{8,12},{1,5},{5,9},{9,13},{2,6},{6,10},{10,14},{3,7},{... | collective-permute-start | bytes 98312 | tf_op jit(solution)/shard_map/ppermute | solution.py:19
  149.1 46.9 %collective-permute-start.29 = (bf16[1,1,128,128]{3,2,1,0:T(8,128)(2,1)S(1)}, bf16[1,1,128,128]{3,2,1,0:T(8,128)(2,1)S(1)}, u32[]{:S(2)}, u32[]{:S(2)}) collective-permute-start(bf16[1,1,128,128]{3,2,1,0:T(8,128)(2,1)S(1)} %get-tuple-element.47), channel_id=1, source_target_pairs={{4,0},{8,4},{12,8},{5,1},{9,5},{13,9},{6,2},{10,6},{14,10},{7,3},{... | collective-permute-start | bytes 98312 | tf_op jit(solution)/shard_map/ppermute | solution.py:21
  196.0 3.7 %collective-permute-start.30 = (bf16[1,18,1,128]{3,2,1,0:T(2,128)(2,1)S(1)}, bf16[1,18,1,128]{3,2,1,0:T(2,128)(2,1)S(1)}, u32[]{:S(2)}, u32[]{:S(2)}) collective-permute-start(bf16[1,18,1,128]{3,2,1,0:T(2,128)(2,1)S(1)} %get-tuple-element.37), channel_id=1, source_target_pairs={{1,0},{2,1},{3,2},{0,3},{5,4},{6,5},{7,6},{4,7},{9,8},{10,9},{11,1... | collective-permute-start | bytes 13832 | tf_op jit(solution)/shard_map/ppermute | solution.py:21
  198.3 5.5 %collective-permute-start.31 = (bf16[1,18,1,128]{3,2,1,0:T(2,128)(2,1)S(1)}, bf16[1,18,1,128]{3,2,1,0:T(2,128)(2,1)S(1)}, u32[]{:S(2)}, u32[]{:S(2)}) collective-permute-start(bf16[1,18,1,128]{3,2,1,0:T(2,128)(2,1)S(1)} %get-tuple-element.38), channel_id=1, source_target_pairs={{0,1},{1,2},{2,3},{3,0},{4,5},{5,6},{6,7},{7,4},{8,9},{9,10},{10,1... | collective-permute-start | bytes 13832 | tf_op jit(solution)/shard_map/ppermute | solution.py:19
Sparse Core Ops, SparseCore 0:
  147.0 57.9 reduce-scatter.1
where the time goes:
time: 227 us; the launch traced here: 225 us
  blocking collectives  91.5 us (40%)
  starting transfers between devices  60.1 us (26%)
  waiting for transfers between devices  23.7 us (10%)
  other arithmetic  18.9 us (8%)
  between operations  15.9 us (7%)
  matrix products  9.55 us (4%)
  local copies, waits for them, and re-layouts  5.66 us (2%)
    psum x1, blocking collectives, shards(): lax.psum((local_bias, local_proj), ('dp', 'lat', 'lon'))  45 us
    psum x1, blocking collectives, shards(): lax.psum((jnp.sum(mask_float), jnp.sum(mask_float * surface_cotangent, ax...  36.6 us
    ppermute x16, starting transfers between devices, extended(): lax.ppermute(head, axis, [((i + 1) % count, i) for i in range(ends)])  32.9 us
    ppermute x16, starting transfers between devices, extended(): lax.ppermute(tail, axis, [(i, (i + 1) % count) for i in range(ends)])  27.1 us
    ppermute x16, waiting for transfers between devices, extended(): lax.ppermute(tail, axis, [(i, (i + 1) % count) for i in range(ends)])  11.9 us
    ppermute x16, waiting for transfers between devices, extended(): lax.ppermute(head, axis, [((i + 1) % count, i) for i in range(ends)])  11.7 us
    psum x1, blocking collectives, shards(): own_weight = lax.psum(spatial, 'dp')  9.87 us
    add x4, other arithmetic, solve_steps(): direction = residual + step_beta[turn_index] * direction  5.32 us
  transfers between devices with their start and end apart: 33, of which 12 were waited for; matrix products, arithmetic and copies ran while one was open for 8% of the time, Pallas kernels for 0%

commit v1 on v0

--- a/solution.py
+++ b/solution.py
@@ -6,6 +6,11 @@
 
 ITERS = 6
 helm_coef = 0.5
+
+
+def by_each_axis(value, first, second):
+    half = lax.psum(value, first)
+    return lax.psum(half, second)
 
 
 def extended(cells, sides, width, closed):
@@ -72,8 +77,8 @@
 ):
     samples, lat_rows, lon_cols, channels = hidden_in.shape
     mask_float = sea_mask.astype(jnp.float32)
-    counted, summed = lax.psum(
-        (jnp.sum(mask_float), jnp.sum(mask_float * surface_cotangent, axis=(1, 2))), ("lat", "lon")
+    counted, summed = by_each_axis(
+        (jnp.sum(mask_float), jnp.sum(mask_float * surface_cotangent, axis=(1, 2))), "lon", "lat"
     )
     adjoint_start = mask_float * (surface_cotangent - (summed / counted)[:, None, None])
     coefs = jnp.stack([mask_float, ocean_depth])

time: 227 us -> 212 us (0.934)
  blocking collectives: 91.5 us -> 76.5 us
    psum x1 -> x2, blocking collectives: 36.6 us -> 21.6 us  [the longest x1 13.4 us: by_each_axis(): half = lax.psum(value, first)]
where the time goes in v1:
time: 212 us; the launch traced here: 211 us
  blocking collectives  76.5 us (36%)
  starting transfers between devices  61 us (29%)
  waiting for transfers between devices  23.2 us (11%)
  other arithmetic  18.8 us (9%)
  between operations  15.9 us (8%)
  matrix products  9.56 us (5%)
  local copies, waits for them, and re-layouts  5.63 us (3%)
    psum x1, blocking collectives, shards(): lax.psum((local_bias, local_proj), ('dp', 'lat', 'lon'))  45 us
    ppermute x16, starting transfers between devices, extended(): lax.ppermute(head, axis, [((i + 1) % count, i) for i in range(ends)])  32.8 us
    ppermute x16, starting transfers between devices, extended(): lax.ppermute(tail, axis, [(i, (i + 1) % count) for i in range(ends)])  28.1 us
    psum x1, blocking collectives, by_each_axis(): half = lax.psum(value, first)  13.4 us
    ppermute x16, waiting for transfers between devices, extended(): lax.ppermute(tail, axis, [(i, (i + 1) % count) for i in range(ends)])  11.9 us
    ppermute x16, waiting for transfers between devices, extended(): lax.ppermute(head, axis, [((i + 1) % count, i) for i in range(ends)])  11.3 us
    psum x1, blocking collectives, shards(): own_weight = lax.psum(spatial, 'dp')  9.88 us
    psum x1, blocking collectives, by_each_axis(): return lax.psum(half, second)  8.21 us
  transfers between devices with their start and end apart: 33, of which 12 were waited for; matrix products, arithmetic and copies ran while one was open for 8% of the time, Pallas kernels for 0%

profile of v1, /device:TPU:0, one launch (start us, length us, event | category | flops | bytes accessed | tf_op | source)
XLA Modules:
  0.0 210.6 jit_solution(14255143070344174793)
XLA Ops:
  8.7 2.4 %collective-permute-start = (f32[2,1,128]{2,1,0:T(1,128)S(1)}, f32[2,1,128]{2,1,0:T(1,128)S(1)}, u32[]{:S(2)}, u32[]{:S(2)}) collective-permute-start(f32[2,1,128]{2,1,0:T(1,128)S(1)} %get-tuple-element.59), channel_id=1, source_target_pairs={{0,4},{4,8},{8,12},{1,5},{5,9},{9,13},{2,6},{6,10},{10,14},{3,7},{... | collective-permute-start | bytes 3080 | tf_op jit(solution)/shard_map/ppermute | solution.py:24
  11.1 1.3 collective-permute-start.1
  12.4 1.3 convert_reduce_fusion.1
  13.7 1.3 multiply_reduce_fusion.1
  15.0 13.4 %all-reduce.1 = (f32[1]{0:T(128)}, f32[]{:T(128)}) all-reduce(f32[1]{0:T(128)} %bitcast.2, f32[]{:T(128)} %convert_reduce_fusion.1), channel_id=1, replica_groups=mesh['dp'=2,'lat'=4,'lon'=4] {'lon'}, use_global_device_ids=true, to_apply=%region_1.0 | all-reduce | flops 2 | bytes 16 | tf_op jit(solution)/shard_map/psum | solution.py:12
  28.4 8.2 %all-reduce.2 = (f32[1]{0:T(128)}, f32[1]{0:T(128)}) all-reduce(f32[1]{0:T(128)} %get-tuple-element.6, f32[1]{0:T(128)} %bitcast.3), channel_id=1, replica_groups=mesh['dp'=2,'lat'=4,'lon'=4] {'lat'}, use_global_device_ids=true, to_apply=%region_2.0 | all-reduce | flops 2 | bytes 16 | tf_op jit(solution)/shard_map/psum | solution.py:13
  38.7 2.2 %collective-permute-start.4 = (f32[1,1,128]{2,1,0:T(1,128)S(1)}, f32[1,1,128]{2,1,0:T(1,128)S(1)}, u32[]{:S(2)}, u32[]{:S(2)}) collective-permute-start(f32[1,1,128]{2,1,0:T(1,128)S(1)} %get-tuple-element.79), channel_id=1, source_target_pairs={{0,4},{4,8},{8,12},{1,5},{5,9},{9,13},{2,6},{6,10},{10,14},{3,7},{... | collective-permute-start | bytes 1544 | tf_op jit(solution)/shard_map/ppermute | solution.py:24
  40.9 1.3 collective-permute-start.5
  42.2 1.5 fusion.171
  43.8 1.4 fusion.172
  46.5 3.7 %collective-permute-start.3 = (f32[2,18,1]{2,1,0:T(8,128)S(1)}, f32[2,18,1]{2,1,0:T(8,128)S(1)}, u32[]{:S(2)}, u32[]{:S(2)}) collective-permute-start(f32[2,18,1]{2,1,0:T(8,128)S(1)} %get-tuple-element.58), channel_id=1, source_target_pairs={{1,0},{2,1},{3,2},{0,3},{5,4},{6,5},{7,6},{4,7},{9,8},{10,9},{11,1... | collective-permute-start | bytes 440 | tf_op jit(solution)/shard_map/ppermute | solution.py:26
  50.2 2.0 collective-permute-start.7
  53.9 1.4 multiply_add_fusion.3
  55.3 2.5 %collective-permute-start.8 = (f32[1,1,128]{2,1,0:T(1,128)S(1)}, f32[1,1,128]{2,1,0:T(1,128)S(1)}, u32[]{:S(2)}, u32[]{:S(2)}) collective-permute-start(f32[1,1,128]{2,1,0:T(1,128)S(1)} %get-tuple-element.77), channel_id=1, source_target_pairs={{0,4},{4,8},{8,12},{1,5},{5,9},{9,13},{2,6},{6,10},{10,14},{3,7},{... | collective-permute-start | bytes 1544 | tf_op jit(solution)/shard_map/ppermute | solution.py:24
  57.9 1.3 collective-permute-start.9
  59.2 4.7 %collective-permute-done.9 = f32[1,1,128]{2,1,0:T(1,128)S(1)} collective-permute-done((f32[1,1,128]{2,1,0:T(1,128)S(1)}, f32[1,1,128]{2,1,0:T(1,128)S(1)}, u32[]{:S(2)}, u32[]{:S(2)}) %collective-permute-start.9) | collective-permute-done | bytes 544 | tf_op jit(solution)/shard_map/ppermute | solution.py:26
  64.0 3.8 %collective-permute-start.11 = (f32[1,18,1]{2,1,0:T(8,128)S(1)}, f32[1,18,1]{2,1,0:T(8,128)S(1)}, u32[]{:S(2)}, u32[]{:S(2)}) collective-permute-start(f32[1,18,1]{2,1,0:T(8,128)S(1)} %get-tuple-element.68), channel_id=1, source_target_pairs={{1,0},{2,1},{3,2},{0,3},{5,4},{6,5},{7,6},{4,7},{9,8},{10,9},{11,1... | collective-permute-start | bytes 224 | tf_op jit(solution)/shard_map/ppermute | solution.py:26
  67.8 1.7 collective-permute-done.10
  69.4 1.4 multiply_add_fusion.2
  70.8 3.3 %collective-permute-start.12 = (f32[1,1,128]{2,1,0:T(1,128)S(1)}, f32[1,1,128]{2,1,0:T(1,128)S(1)}, u32[]{:S(2)}, u32[]{:S(2)}) collective-permute-start(f32[1,1,128]{2,1,0:T(1,128)S(1)} %get-tuple-element.75), channel_id=1, source_target_pairs={{0,4},{4,8},{8,12},{1,5},{5,9},{9,13},{2,6},{6,10},{10,14},{3,7},{... | collective-permute-start | bytes 1544 | tf_op jit(solution)/shard_map/ppermute | solution.py:24
  74.1 1.3 collective-permute-start.13
  75.4 2.2 %collective-permute-done.13 = f32[1,1,128]{2,1,0:T(1,128)S(1)} collective-permute-done((f32[1,1,128]{2,1,0:T(1,128)S(1)}, f32[1,1,128]{2,1,0:T(1,128)S(1)}, u32[]{:S(2)}, u32[]{:S(2)}) %collective-permute-start.13) | collective-permute-done | bytes 544 | tf_op jit(solution)/shard_map/ppermute | solution.py:26
  78.8 2.8 %collective-permute-start.15 = (f32[1,18,1]{2,1,0:T(8,128)S(1)}, f32[1,18,1]{2,1,0:T(8,128)S(1)}, u32[]{:S(2)}, u32[]{:S(2)}) collective-permute-start(f32[1,18,1]{2,1,0:T(8,128)S(1)} %get-tuple-element.66), channel_id=1, source_target_pairs={{1,0},{2,1},{3,2},{0,3},{5,4},{6,5},{7,6},{4,7},{9,8},{10,9},{11,1... | collective-permute-start | bytes 224 | tf_op jit(solution)/shard_map/ppermute | solution.py:26
  81.6 1.6 collective-permute-done.14
  83.2 1.4 multiply_add_fusion.1
  84.6 3.4 %collective-permute-start.16 = (f32[1,1,128]{2,1,0:T(1,128)S(1)}, f32[1,1,128]{2,1,0:T(1,128)S(1)}, u32[]{:S(2)}, u32[]{:S(2)}) collective-permute-start(f32[1,1,128]{2,1,0:T(1,128)S(1)} %get-tuple-element.73), channel_id=1, source_target_pairs={{0,4},{4,8},{8,12},{1,5},{5,9},{9,13},{2,6},{6,10},{10,14},{3,7},{... | collective-permute-start | bytes 1544 | tf_op jit(solution)/shard_map/ppermute | solution.py:24
  88.0 1.3 collective-permute-start.17
  89.3 2.2 %collective-permute-done.17 = f32[1,1,128]{2,1,0:T(1,128)S(1)} collective-permute-done((f32[1,1,128]{2,1,0:T(1,128)S(1)}, f32[1,1,128]{2,1,0:T(1,128)S(1)}, u32[]{:S(2)}, u32[]{:S(2)}) %collective-permute-start.17) | collective-permute-done | bytes 544 | tf_op jit(solution)/shard_map/ppermute | solution.py:26
  91.5 1.3 collective-permute-start.18
  92.8 2.6 %collective-permute-start.19 = (f32[1,18,1]{2,1,0:T(8,128)S(1)}, f32[1,18,1]{2,1,0:T(8,128)S(1)}, u32[]{:S(2)}, u32[]{:S(2)}) collective-permute-start(f32[1,18,1]{2,1,0:T(8,128)S(1)} %get-tuple-element.64), channel_id=1, source_target_pairs={{1,0},{2,1},{3,2},{0,3},{5,4},{6,5},{7,6},{4,7},{9,8},{10,9},{11,1... | collective-permute-start | bytes 224 | tf_op jit(solution)/shard_map/ppermute | solution.py:26
  95.5 1.6 collective-permute-done.18
  98.3 3.4 %collective-permute-start.20 = (f32[1,1,128]{2,1,0:T(1,128)S(1)}, f32[1,1,128]{2,1,0:T(1,128)S(1)}, u32[]{:S(2)}, u32[]{:S(2)}) collective-permute-start(f32[1,1,128]{2,1,0:T(1,128)S(1)} %get-tuple-element.71), channel_id=1, source_target_pairs={{0,4},{4,8},{8,12},{1,5},{5,9},{9,13},{2,6},{6,10},{10,14},{3,7},{... | collective-permute-start | bytes 1544 | tf_op jit(solution)/shard_map/ppermute | solution.py:24
  101.7 1.3 collective-permute-start.21
  103.0 3.5 %collective-permute-start.24 = (bf16[1,1,128,128]{3,2,1,0:T(8,128)(2,1)S(1)}, bf16[1,1,128,128]{3,2,1,0:T(8,128)(2,1)S(1)}, u32[]{:S(2)}, u32[]{:S(2)}) collective-permute-start(bf16[1,1,128,128]{3,2,1,0:T(8,128)(2,1)S(1)} %get-tuple-element.54), channel_id=1, source_target_pairs={{0,4},{4,8},{8,12},{1,5},{5,9},{9,13},{2,6},{6,10},{10,14},{3,7},{... | collective-permute-start | bytes 98312 | tf_op jit(solution)/shard_map/ppermute | solution.py:24
  106.4 1.3 collective-permute-start.25
  107.9 1.3 collective-permute-start.22
  109.2 2.6 %collective-permute-start.23 = (f32[1,18,1]{2,1,0:T(8,128)S(1)}, f32[1,18,1]{2,1,0:T(8,128)S(1)}, u32[]{:S(2)}, u32[]{:S(2)}) collective-permute-start(f32[1,18,1]{2,1,0:T(8,128)S(1)} %get-tuple-element.62), channel_id=1, source_target_pairs={{1,0},{2,1},{3,2},{0,3},{5,4},{6,5},{7,6},{4,7},{9,8},{10,9},{11,1... | collective-permute-start | bytes 224 | tf_op jit(solution)/shard_map/ppermute | solution.py:26
  111.8 1.6 collective-permute-done.22
  113.4 4.4 %fusion.69 = f32[2048]{0:T(1024)S(1)} fusion(f32[1,16,128]{2,1,0:T(8,128)S(1)} %get-tuple-element.13, f32[1,16,128]{2,1,0:T(8,128)S(1)} %get-tuple-element.23, f32[1,16,128]{2,1,0:T(8,128)S(1)} %get-tuple-element.12, f32[1,18,1]{2,1,0:T(8,128)S(1)} %collective-permute-done.23, f32[1,1,128]{2,1,0:T(1,128)S(1)} %collective-permute-done.21, ...), kind=kLoop, calls=%fused_computation.128 | loop fusion | flops 79872 | bytes 107692 | tf_op jit(solution)/shard_map/mul | solution.py:110
  118.2 1.4 collective-permute-start.26
  119.6 2.6 %collective-permute-start.27 = (bf16[1,18,1,128]{3,2,1,0:T(2,128)(2,1)S(1)}, bf16[1,18,1,128]{3,2,1,0:T(2,128)(2,1)S(1)}, u32[]{:S(2)}, u32[]{:S(2)}) collective-permute-start(bf16[1,18,1,128]{3,2,1,0:T(2,128)(2,1)S(1)} %get-tuple-element.45), channel_id=1, source_target_pairs={{1,0},{2,1},{3,2},{0,3},{5,4},{6,5},{7,6},{4,7},{9,8},{10,9},{11,1... | collective-permute-start | bytes 13832 | tf_op jit(solution)/shard_map/ppermute | solution.py:26
  122.5 1.3 collective-permute-done.26
  132.3 2.2 %collective-permute-start.28 = (bf16[1,1,128,128]{3,2,1,0:T(8,128)(2,1)S(1)}, bf16[1,1,128,128]{3,2,1,0:T(8,128)(2,1)S(1)}, u32[]{:S(2)}, u32[]{:S(2)}) collective-permute-start(bf16[1,1,128,128]{3,2,1,0:T(8,128)(2,1)S(1)} %get-tuple-element.48), channel_id=1, source_target_pairs={{0,4},{4,8},{8,12},{1,5},{5,9},{9,13},{2,6},{6,10},{10,14},{3,7},{... | collective-permute-start | bytes 98312 | tf_op jit(solution)/shard_map/ppermute | solution.py:24
  134.5 1.3 collective-permute-start.29
  135.8 45.0 %all-reduce = (f32[128]{0:T(128)S(1)}, f32[128]{0:T(128)S(1)}) all-reduce(f32[128]{0:T(128)S(1)} %get-tuple-element.10, f32[128]{0:T(128)S(1)} %get-tuple-element.24), channel_id=1, replica_groups=mesh['dp'=2,'lat'=4,'lon'=4] {'dp','lat','lon'}, use_global_device_ids=true, to_apply=%region_9.0 | all-reduce | flops 256 | bytes 2048 | tf_op jit(solution)/shard_map/psum | solution.py:145
  181.4 2.3 %collective-permute-start.30 = (bf16[1,18,1,128]{3,2,1,0:T(2,128)(2,1)S(1)}, bf16[1,18,1,128]{3,2,1,0:T(2,128)(2,1)S(1)}, u32[]{:S(2)}, u32[]{:S(2)}) collective-permute-start(bf16[1,18,1,128]{3,2,1,0:T(2,128)(2,1)S(1)} %get-tuple-element.39), channel_id=1, source_target_pairs={{1,0},{2,1},{3,2},{0,3},{5,4},{6,5},{7,6},{4,7},{9,8},{10,9},{11,1... | collective-permute-start | bytes 13832 | tf_op jit(solution)/shard_map/ppermute | solution.py:26
  185.1 4.1 %collective-permute-done.31 = bf16[1,18,1,128]{3,2,1,0:T(2,128)(2,1)S(1)} collective-permute-done((bf16[1,18,1,128]{3,2,1,0:T(2,128)(2,1)S(1)}, bf16[1,18,1,128]{3,2,1,0:T(2,128)(2,1)S(1)}, u32[]{:S(2)}, u32[]{:S(2)}) %collective-permute-start.31) | collective-permute-done | bytes 4640 | tf_op jit(solution)/shard_map/ppermute | solution.py:24
  193.3 9.9 %psum.53 = f32[8,3,3,128]{3,0,2,1:T(8,128)S(1)} all-reduce(f32[8,3,3,128]{3,0,2,1:T(8,128)} %reduce-scatter.2.cloned.1.call-done), channel_id=1, replica_groups=mesh['dp'=2,'lat'=4,'lon'=4] {'dp'}, use_global_device_ids=true, to_apply=%region_7.0 | all-reduce | flops 9216 | bytes 73728 | tf_op jit(solution)/shard_map/psum | solution.py:144
  (106 shorter events, 23.4 us)
Async XLA Ops:
  7.2 106.2 %copy-start.3 = (s32[16,128]{1,0:T(8,128)S(1)}, s32[16,128]{1,0:T(8,128)}, u32[]{:S(2)}) copy-start(s32[16,128]{1,0:T(8,128)} %param.14) | copy-start | bytes 24580
  7.2 95.8 %copy-start = (bf16[1,16,128,128]{3,2,1,0:T(8,128)(2,1)S(1)}, bf16[1,16,128,128]{3,2,1,0:T(8,128)(2,1)}, u32[]{:S(2)}) copy-start(bf16[1,16,128,128]{3,2,1,0:T(8,128)(2,1)} %param.9) | copy-start | bytes 1572868
  7.2 186.1 %reduce-scatter.2.cloned.1.call-start = ((), (), s32[]{:S(2)}) async-start(), calls=%async_computation.1 | async-start | bytes 626688 | tf_op jit(solution)/shard_map/reduce_scatter | solution.py:138
  8.7 36.9 %collective-permute-start = (f32[2,1,128]{2,1,0:T(1,128)S(1)}, f32[2,1,128]{2,1,0:T(1,128)S(1)}, u32[]{:S(2)}, u32[]{:S(2)}) collective-permute-start(f32[2,1,128]{2,1,0:T(1,128)S(1)} %get-tuple-element.59), channel_id=1, source_target_pairs={{0,4},{4,8},{8,12},{1,5},{5,9},{9,13},{2,6},{6,10},{10,14},{3,7},{... | collective-permute-start | bytes 3080 | tf_op jit(solution)/shard_map/ppermute | solution.py:24
  11.1 34.5 %collective-permute-start.1 = (f32[2,1,128]{2,1,0:T(1,128)S(1)}, f32[2,1,128]{2,1,0:T(1,128)S(1)}, u32[]{:S(2)}, u32[]{:S(2)}) collective-permute-start(f32[2,1,128]{2,1,0:T(1,128)S(1)} %get-tuple-element.60), channel_id=1, source_target_pairs={{4,0},{8,4},{12,8},{5,1},{9,5},{13,9},{6,2},{10,6},{14,10},{7,3},{... | collective-permute-start | bytes 3080 | tf_op jit(solution)/shard_map/ppermute | solution.py:26
  38.7 6.5 %collective-permute-start.4 = (f32[1,1,128]{2,1,0:T(1,128)S(1)}, f32[1,1,128]{2,1,0:T(1,128)S(1)}, u32[]{:S(2)}, u32[]{:S(2)}) collective-permute-start(f32[1,1,128]{2,1,0:T(1,128)S(1)} %get-tuple-element.79), channel_id=1, source_target_pairs={{0,4},{4,8},{8,12},{1,5},{5,9},{9,13},{2,6},{6,10},{10,14},{3,7},{... | collective-permute-start | bytes 1544 | tf_op jit(solution)/shard_map/ppermute | solution.py:24
  40.9 4.5 %collective-permute-start.5 = (f32[1,1,128]{2,1,0:T(1,128)S(1)}, f32[1,1,128]{2,1,0:T(1,128)S(1)}, u32[]{:S(2)}, u32[]{:S(2)}) collective-permute-start(f32[1,1,128]{2,1,0:T(1,128)S(1)} %get-tuple-element.80), channel_id=1, source_target_pairs={{4,0},{8,4},{12,8},{5,1},{9,5},{13,9},{6,2},{10,6},{14,10},{7,3},{... | collective-permute-start | bytes 1544 | tf_op jit(solution)/shard_map/ppermute | solution.py:26
  45.5 7.5 %collective-permute-start.6 = (f32[1,18,1]{2,1,0:T(8,128)S(1)}, f32[1,18,1]{2,1,0:T(8,128)S(1)}, u32[]{:S(2)}, u32[]{:S(2)}) collective-permute-start(f32[1,18,1]{2,1,0:T(8,128)S(1)} %get-tuple-element.69), channel_id=1, source_target_pairs={{0,1},{1,2},{2,3},{3,0},{4,5},{5,6},{6,7},{7,4},{8,9},{9,10},{10,1... | collective-permute-start | bytes 224 | tf_op jit(solution)/shard_map/ppermute | solution.py:24
  46.4 5.8 %collective-permute-start.2 = (f32[2,18,1]{2,1,0:T(8,128)S(1)}, f32[2,18,1]{2,1,0:T(8,128)S(1)}, u32[]{:S(2)}, u32[]{:S(2)}) collective-permute-start(f32[2,18,1]{2,1,0:T(8,128)S(1)} %get-tuple-element.57), channel_id=1, source_target_pairs={{0,1},{1,2},{2,3},{3,0},{4,5},{5,6},{6,7},{7,4},{8,9},{9,10},{10,1... | collective-permute-start | bytes 440 | tf_op jit(solution)/shard_map/ppermute | solution.py:24
  46.5 5.7 %collective-permute-start.3 = (f32[2,18,1]{2,1,0:T(8,128)S(1)}, f32[2,18,1]{2,1,0:T(8,128)S(1)}, u32[]{:S(2)}, u32[]{:S(2)}) collective-permute-start(f32[2,18,1]{2,1,0:T(8,128)S(1)} %get-tuple-element.58), channel_id=1, source_target_pairs={{1,0},{2,1},{3,2},{0,3},{5,4},{6,5},{7,6},{4,7},{9,8},{10,9},{11,1... | collective-permute-start | bytes 440 | tf_op jit(solution)/shard_map/ppermute | solution.py:26
  50.2 3.7 %collective-permute-start.7 = (f32[1,18,1]{2,1,0:T(8,128)S(1)}, f32[1,18,1]{2,1,0:T(8,128)S(1)}, u32[]{:S(2)}, u32[]{:S(2)}) collective-permute-start(f32[1,18,1]{2,1,0:T(8,128)S(1)} %get-tuple-element.70), channel_id=1, source_target_pairs={{1,0},{2,1},{3,2},{0,3},{5,4},{6,5},{7,6},{4,7},{9,8},{10,9},{11,1... | collective-permute-start | bytes 224 | tf_op jit(solution)/shard_map/ppermute | solution.py:26
  55.3 3.9 %collective-permute-start.8 = (f32[1,1,128]{2,1,0:T(1,128)S(1)}, f32[1,1,128]{2,1,0:T(1,128)S(1)}, u32[]{:S(2)}, u32[]{:S(2)}) collective-permute-start(f32[1,1,128]{2,1,0:T(1,128)S(1)} %get-tuple-element.77), channel_id=1, source_target_pairs={{0,4},{4,8},{8,12},{1,5},{5,9},{9,13},{2,6},{6,10},{10,14},{3,7},{... | collective-permute-start | bytes 1544 | tf_op jit(solution)/shard_map/ppermute | solution.py:24
  57.9 6.0 %collective-permute-start.9 = (f32[1,1,128]{2,1,0:T(1,128)S(1)}, f32[1,1,128]{2,1,0:T(1,128)S(1)}, u32[]{:S(2)}, u32[]{:S(2)}) collective-permute-start(f32[1,1,128]{2,1,0:T(1,128)S(1)} %get-tuple-element.78), channel_id=1, source_target_pairs={{4,0},{8,4},{12,8},{5,1},{9,5},{13,9},{6,2},{10,6},{14,10},{7,3},{... | collective-permute-start | bytes 1544 | tf_op jit(solution)/shard_map/ppermute | solution.py:26
  63.9 5.5 %collective-permute-start.10 = (f32[1,18,1]{2,1,0:T(8,128)S(1)}, f32[1,18,1]{2,1,0:T(8,128)S(1)}, u32[]{:S(2)}, u32[]{:S(2)}) collective-permute-start(f32[1,18,1]{2,1,0:T(8,128)S(1)} %get-tuple-element.67), channel_id=1, source_target_pairs={{0,1},{1,2},{2,3},{3,0},{4,5},{5,6},{6,7},{7,4},{8,9},{9,10},{10,1... | collective-permute-start | bytes 224 | tf_op jit(solution)/shard_map/ppermute | solution.py:24
  64.0 5.5 %collective-permute-start.11 = (f32[1,18,1]{2,1,0:T(8,128)S(1)}, f32[1,18,1]{2,1,0:T(8,128)S(1)}, u32[]{:S(2)}, u32[]{:S(2)}) collective-permute-start(f32[1,18,1]{2,1,0:T(8,128)S(1)} %get-tuple-element.68), channel_id=1, source_target_pairs={{1,0},{2,1},{3,2},{0,3},{5,4},{6,5},{7,6},{4,7},{9,8},{10,9},{11,1... | collective-permute-start | bytes 224 | tf_op jit(solution)/shard_map/ppermute | solution.py:26
  70.8 4.6 %collective-permute-start.12 = (f32[1,1,128]{2,1,0:T(1,128)S(1)}, f32[1,1,128]{2,1,0:T(1,128)S(1)}, u32[]{:S(2)}, u32[]{:S(2)}) collective-permute-start(f32[1,1,128]{2,1,0:T(1,128)S(1)} %get-tuple-element.75), channel_id=1, source_target_pairs={{0,4},{4,8},{8,12},{1,5},{5,9},{9,13},{2,6},{6,10},{10,14},{3,7},{... | collective-permute-start | bytes 1544 | tf_op jit(solution)/shard_map/ppermute | solution.py:24
  74.1 3.5 %collective-permute-start.13 = (f32[1,1,128]{2,1,0:T(1,128)S(1)}, f32[1,1,128]{2,1,0:T(1,128)S(1)}, u32[]{:S(2)}, u32[]{:S(2)}) collective-permute-start(f32[1,1,128]{2,1,0:T(1,128)S(1)} %get-tuple-element.76), channel_id=1, source_target_pairs={{4,0},{8,4},{12,8},{5,1},{9,5},{13,9},{6,2},{10,6},{14,10},{7,3},{... | collective-permute-start | bytes 1544 | tf_op jit(solution)/shard_map/ppermute | solution.py:26
  77.7 5.5 %collective-permute-start.14 = (f32[1,18,1]{2,1,0:T(8,128)S(1)}, f32[1,18,1]{2,1,0:T(8,128)S(1)}, u32[]{:S(2)}, u32[]{:S(2)}) collective-permute-start(f32[1,18,1]{2,1,0:T(8,128)S(1)} %get-tuple-element.65), channel_id=1, source_target_pairs={{0,1},{1,2},{2,3},{3,0},{4,5},{5,6},{6,7},{7,4},{8,9},{9,10},{10,1... | collective-permute-start | bytes 224 | tf_op jit(solution)/shard_map/ppermute | solution.py:24
  78.8 4.4 %collective-permute-start.15 = (f32[1,18,1]{2,1,0:T(8,128)S(1)}, f32[1,18,1]{2,1,0:T(8,128)S(1)}, u32[]{:S(2)}, u32[]{:S(2)}) collective-permute-start(f32[1,18,1]{2,1,0:T(8,128)S(1)} %get-tuple-element.66), channel_id=1, source_target_pairs={{1,0},{2,1},{3,2},{0,3},{5,4},{6,5},{7,6},{4,7},{9,8},{10,9},{11,1... | collective-permute-start | bytes 224 | tf_op jit(solution)/shard_map/ppermute | solution.py:26
  84.6 4.7 %collective-permute-start.16 = (f32[1,1,128]{2,1,0:T(1,128)S(1)}, f32[1,1,128]{2,1,0:T(1,128)S(1)}, u32[]{:S(2)}, u32[]{:S(2)}) collective-permute-start(f32[1,1,128]{2,1,0:T(1,128)S(1)} %get-tuple-element.73), channel_id=1, source_target_pairs={{0,4},{4,8},{8,12},{1,5},{5,9},{9,13},{2,6},{6,10},{10,14},{3,7},{... | collective-permute-start | bytes 1544 | tf_op jit(solution)/shard_map/ppermute | solution.py:24
  88.0 3.5 %collective-permute-start.17 = (f32[1,1,128]{2,1,0:T(1,128)S(1)}, f32[1,1,128]{2,1,0:T(1,128)S(1)}, u32[]{:S(2)}, u32[]{:S(2)}) collective-permute-start(f32[1,1,128]{2,1,0:T(1,128)S(1)} %get-tuple-element.74), channel_id=1, source_target_pairs={{4,0},{8,4},{12,8},{5,1},{9,5},{13,9},{6,2},{10,6},{14,10},{7,3},{... | collective-permute-start | bytes 1544 | tf_op jit(solution)/shard_map/ppermute | solution.py:26
  91.5 5.5 %collective-permute-start.18 = (f32[1,18,1]{2,1,0:T(8,128)S(1)}, f32[1,18,1]{2,1,0:T(8,128)S(1)}, u32[]{:S(2)}, u32[]{:S(2)}) collective-permute-start(f32[1,18,1]{2,1,0:T(8,128)S(1)} %get-tuple-element.63), channel_id=1, source_target_pairs={{0,1},{1,2},{2,3},{3,0},{4,5},{5,6},{6,7},{7,4},{8,9},{9,10},{10,1... | collective-permute-start | bytes 224 | tf_op jit(solution)/shard_map/ppermute | solution.py:24
  92.8 4.2 %collective-permute-start.19 = (f32[1,18,1]{2,1,0:T(8,128)S(1)}, f32[1,18,1]{2,1,0:T(8,128)S(1)}, u32[]{:S(2)}, u32[]{:S(2)}) collective-permute-start(f32[1,18,1]{2,1,0:T(8,128)S(1)} %get-tuple-element.64), channel_id=1, source_target_pairs={{1,0},{2,1},{3,2},{0,3},{5,4},{6,5},{7,6},{4,7},{9,8},{10,9},{11,1... | collective-permute-start | bytes 224 | tf_op jit(solution)/shard_map/ppermute | solution.py:26
  98.3 9.5 %collective-permute-start.20 = (f32[1,1,128]{2,1,0:T(1,128)S(1)}, f32[1,1,128]{2,1,0:T(1,128)S(1)}, u32[]{:S(2)}, u32[]{:S(2)}) collective-permute-start(f32[1,1,128]{2,1,0:T(1,128)S(1)} %get-tuple-element.71), channel_id=1, source_target_pairs={{0,4},{4,8},{8,12},{1,5},{5,9},{9,13},{2,6},{6,10},{10,14},{3,7},{... | collective-permute-start | bytes 1544 | tf_op jit(solution)/shard_map/ppermute | solution.py:24
  101.7 6.1 %collective-permute-start.21 = (f32[1,1,128]{2,1,0:T(1,128)S(1)}, f32[1,1,128]{2,1,0:T(1,128)S(1)}, u32[]{:S(2)}, u32[]{:S(2)}) collective-permute-start(f32[1,1,128]{2,1,0:T(1,128)S(1)} %get-tuple-element.72), channel_id=1, source_target_pairs={{4,0},{8,4},{12,8},{5,1},{9,5},{13,9},{6,2},{10,6},{14,10},{7,3},{... | collective-permute-start | bytes 1544 | tf_op jit(solution)/shard_map/ppermute | solution.py:26
  103.0 14.8 %collective-permute-start.24 = (bf16[1,1,128,128]{3,2,1,0:T(8,128)(2,1)S(1)}, bf16[1,1,128,128]{3,2,1,0:T(8,128)(2,1)S(1)}, u32[]{:S(2)}, u32[]{:S(2)}) collective-permute-start(bf16[1,1,128,128]{3,2,1,0:T(8,128)(2,1)S(1)} %get-tuple-element.54), channel_id=1, source_target_pairs={{0,4},{4,8},{8,12},{1,5},{5,9},{9,13},{2,6},{6,10},{10,14},{3,7},{... | collective-permute-start | bytes 98312 | tf_op jit(solution)/shard_map/ppermute | solution.py:24
  106.4 11.4 %collective-permute-start.25 = (bf16[1,1,128,128]{3,2,1,0:T(8,128)(2,1)S(1)}, bf16[1,1,128,128]{3,2,1,0:T(8,128)(2,1)S(1)}, u32[]{:S(2)}, u32[]{:S(2)}) collective-permute-start(bf16[1,1,128,128]{3,2,1,0:T(8,128)(2,1)S(1)} %get-tuple-element.53), channel_id=1, source_target_pairs={{4,0},{8,4},{12,8},{5,1},{9,5},{13,9},{6,2},{10,6},{14,10},{7,3},{... | collective-permute-start | bytes 98312 | tf_op jit(solution)/shard_map/ppermute | solution.py:26
  107.9 5.5 %collective-permute-start.22 = (f32[1,18,1]{2,1,0:T(8,128)S(1)}, f32[1,18,1]{2,1,0:T(8,128)S(1)}, u32[]{:S(2)}, u32[]{:S(2)}) collective-permute-start(f32[1,18,1]{2,1,0:T(8,128)S(1)} %get-tuple-element.61), channel_id=1, source_target_pairs={{0,1},{1,2},{2,3},{3,0},{4,5},{5,6},{6,7},{7,4},{8,9},{9,10},{10,1... | collective-permute-start | bytes 224 | tf_op jit(solution)/shard_map/ppermute | solution.py:24
  109.2 4.2 %collective-permute-start.23 = (f32[1,18,1]{2,1,0:T(8,128)S(1)}, f32[1,18,1]{2,1,0:T(8,128)S(1)}, u32[]{:S(2)}, u32[]{:S(2)}) collective-permute-start(f32[1,18,1]{2,1,0:T(8,128)S(1)} %get-tuple-element.62), channel_id=1, source_target_pairs={{1,0},{2,1},{3,2},{0,3},{5,4},{6,5},{7,6},{4,7},{9,8},{10,9},{11,1... | collective-permute-start | bytes 224 | tf_op jit(solution)/shard_map/ppermute | solution.py:26
  117.8 4.4 %copy-start.1 = (bf16[3,3,128,128]{3,2,1,0:T(8,128)(2,1)S(1)}, bf16[3,3,128,128]{3,2,1,0:T(8,128)(2,1)}, u32[]{:S(2)}) copy-start(bf16[3,3,128,128]{3,2,1,0:T(8,128)(2,1)} %param.10) | copy-start | bytes 884740
  118.2 5.6 %collective-permute-start.26 = (bf16[1,18,1,128]{3,2,1,0:T(2,128)(2,1)S(1)}, bf16[1,18,1,128]{3,2,1,0:T(2,128)(2,1)S(1)}, u32[]{:S(2)}, u32[]{:S(2)}) collective-permute-start(bf16[1,18,1,128]{3,2,1,0:T(2,128)(2,1)S(1)} %get-tuple-element.44), channel_id=1, source_target_pairs={{0,1},{1,2},{2,3},{3,0},{4,5},{5,6},{6,7},{7,4},{8,9},{9,10},{10,1... | collective-permute-start | bytes 13832 | tf_op jit(solution)/shard_map/ppermute | solution.py:24
  119.6 4.2 %collective-permute-start.27 = (bf16[1,18,1,128]{3,2,1,0:T(2,128)(2,1)S(1)}, bf16[1,18,1,128]{3,2,1,0:T(2,128)(2,1)S(1)}, u32[]{:S(2)}, u32[]{:S(2)}) collective-permute-start(bf16[1,18,1,128]{3,2,1,0:T(2,128)(2,1)S(1)} %get-tuple-element.45), channel_id=1, source_target_pairs={{1,0},{2,1},{3,2},{0,3},{5,4},{6,5},{7,6},{4,7},{9,8},{10,9},{11,1... | collective-permute-start | bytes 13832 | tf_op jit(solution)/shard_map/ppermute | solution.py:26
  125.0 0.7 copy-start.4
  126.8 0.7 copy-start.5
  131.4 0.8 copy-start.2
  132.3 49.1 %collective-permute-start.28 = (bf16[1,1,128,128]{3,2,1,0:T(8,128)(2,1)S(1)}, bf16[1,1,128,128]{3,2,1,0:T(8,128)(2,1)S(1)}, u32[]{:S(2)}, u32[]{:S(2)}) collective-permute-start(bf16[1,1,128,128]{3,2,1,0:T(8,128)(2,1)S(1)} %get-tuple-element.48), channel_id=1, source_target_pairs={{0,4},{4,8},{8,12},{1,5},{5,9},{9,13},{2,6},{6,10},{10,14},{3,7},{... | collective-permute-start | bytes 98312 | tf_op jit(solution)/shard_map/ppermute | solution.py:24
  134.5 46.9 %collective-permute-start.29 = (bf16[1,1,128,128]{3,2,1,0:T(8,128)(2,1)S(1)}, bf16[1,1,128,128]{3,2,1,0:T(8,128)(2,1)S(1)}, u32[]{:S(2)}, u32[]{:S(2)}) collective-permute-start(bf16[1,1,128,128]{3,2,1,0:T(8,128)(2,1)S(1)} %get-tuple-element.49), channel_id=1, source_target_pairs={{4,0},{8,4},{12,8},{5,1},{9,5},{13,9},{6,2},{10,6},{14,10},{7,3},{... | collective-permute-start | bytes 98312 | tf_op jit(solution)/shard_map/ppermute | solution.py:26
  181.4 3.7 %collective-permute-start.30 = (bf16[1,18,1,128]{3,2,1,0:T(2,128)(2,1)S(1)}, bf16[1,18,1,128]{3,2,1,0:T(2,128)(2,1)S(1)}, u32[]{:S(2)}, u32[]{:S(2)}) collective-permute-start(bf16[1,18,1,128]{3,2,1,0:T(2,128)(2,1)S(1)} %get-tuple-element.39), channel_id=1, source_target_pairs={{1,0},{2,1},{3,2},{0,3},{5,4},{6,5},{7,6},{4,7},{9,8},{10,9},{11,1... | collective-permute-start | bytes 13832 | tf_op jit(solution)/shard_map/ppermute | solution.py:26
  183.7 5.5 %collective-permute-start.31 = (bf16[1,18,1,128]{3,2,1,0:T(2,128)(2,1)S(1)}, bf16[1,18,1,128]{3,2,1,0:T(2,128)(2,1)S(1)}, u32[]{:S(2)}, u32[]{:S(2)}) collective-permute-start(bf16[1,18,1,128]{3,2,1,0:T(2,128)(2,1)S(1)} %get-tuple-element.40), channel_id=1, source_target_pairs={{0,1},{1,2},{2,3},{3,0},{4,5},{5,6},{6,7},{7,4},{8,9},{9,10},{10,1... | collective-permute-start | bytes 13832 | tf_op jit(solution)/shard_map/ppermute | solution.py:24
Sparse Core Ops, SparseCore 0:
  132.4 58.1 reduce-scatter.1
